TPU v7x, 32 devices: a whole 2x2x4 slice. The times are simulated.
32 devices in a mesh: depth: 2 (over core), lat: 16 (over z, y, x).
Axes of the slice: x: 2, y: 2, z: 4, core: 2. Of those that a mesh axis runs over, the one named last changes fastest.
Arguments:
- temp_old: float32 [256, 64, 512], P('depth', 'lat'), may hold values from -6 to 6
- source: float32 [256, 64, 512], P('depth', 'lat'), may hold values from -6 to 6
- lat_couple: float32 [256], P('depth'), may hold values from 0.05 to 0.2
- face_couple: float32 [1], replicated, may hold values from 0.5 to 2
- block_inverse: float32 [256, 128], P('depth'), may hold values from -0.3 to 1.4
Outputs:
- temp_new: float32 [256, 64, 512], P('depth', 'lat')
All inputs are finite; a program needn't handle non-finite values.
Results may differ from a plain program's by a relative error of at most 0.0001.
Values sent between devices are 32-bit elements; how exact they have to be, the bound alone decides.
A program may use at most 64 MiB of HBM per device.

v0:
```python
import jax
import jax.numpy as jnp
from jax import lax
from jax.sharding import PartitionSpec as P

SWEEPS = 6


def shifted(value, axis, steps):
    count = lax.axis_size(axis)
    first, last = (max(0, -steps), min(count, count - steps))
    return lax.ppermute(value, axis, [(source, source + steps) for source in range(first, last)])


def extended(block, sides, width):
    for axis, dim in sides:
        count = lax.axis_size(axis)
        forward = [(i, i + 1) for i in range(count - 1)]
        backward = [(target, source) for source, target in forward]
        low = lax.ppermute(
            lax.slice_in_dim(block, block.shape[dim] - width, None, axis=dim), axis, forward
        )
        high = lax.ppermute(lax.slice_in_dim(block, 0, width, axis=dim), axis, backward)
        block = jnp.concatenate([low, block, high], axis=dim)
    return block


def apply_inverse(inverse, values):
    depth_cells = inverse.shape[0]
    flat = values.reshape(depth_cells, -1)
    return jnp.dot(
        inverse, flat, precision=lax.Precision.HIGHEST, preferred_element_type=jnp.float32
    ).reshape(values.shape)


def across_columns(field):
    padded = jnp.pad(field, ((0, 0), (0, 0), (1, 1)))
    return padded[:, :, 2:] + padded[:, :, :-2]


def local(temp_old, source, lat_couple, face_couple, block_inverse):
    depth_count = lax.axis_size("depth")
    slab_index = lax.axis_index("depth")
    depth_cells, row_count, col_count = temp_old.shape
    couple_above = jnp.where(slab_index > 0, face_couple[jnp.maximum(slab_index - 1, 0)], 0.0)
    couple_below = face_couple[jnp.minimum(slab_index, depth_count - 2)]
    tail_gain = block_inverse[depth_cells - 1, 0] * couple_above
    first_column = block_inverse[:, 0] * couple_above
    weights = lat_couple[:, None, None]
    field = temp_old
    for sweep_index in range(SWEEPS):
        under_layer = shifted(field[0], "depth", -1)
        padded = extended(field, (("lat", 1),), 1)
        across_rows = padded[:, 2:] + padded[:, :-2]
        right_side = source + weights * (across_rows + across_columns(field))
        right_side = right_side.at[depth_cells - 1].add(couple_below * under_layer)
        solved = apply_inverse(block_inverse, right_side)
        bottom = solved[depth_cells - 1]
        incoming = jnp.zeros_like(bottom)
        incoming = shifted(bottom + tail_gain * incoming, "depth", 1)
        field = solved + first_column[:, None, None] * incoming[None]
    return field


def solution(mesh):
    return jax.shard_map(
        local,
        mesh=mesh,
        in_specs=(
            P("depth", "lat", None),
            P("depth", "lat", None),
            P("depth"),
            P(),
            P("depth", None),
        ),
        out_specs=P("depth", "lat", None),
        check_vma=False,
    )
```

profile of v0, /device:TPU:1, one launch (start us, length us, event | category | flops | bytes accessed | tf_op | source)
XLA Modules:
  0.0 153.2 jit_solution(2542641521677961614)
XLA Ops:
  0.0 2.1 %fusion.47 = (f32[128,1,512]{2,1,0:T(1,128)S(1)}, f32[128,1,512]{2,1,0:T(1,128)S(1)}) fusion(f32[128,4,512]{2,1,0:T(4,128)} %param.17), kind=kLoop, calls=%fused_computation.96 | loop fusion | bytes 1048576 | tf_op jit(solution)/shard_map/slice | solution.py:23
  2.1 1.3 collective-permute-start
  3.4 4.6 %collective-permute-start.1 = (f32[128,1,512]{2,1,0:T(1,128)S(1)}, f32[128,1,512]{2,1,0:T(1,128)S(1)}, u32[]{:S(2)}, u32[]{:S(2)}) collective-permute-start(f32[128,1,512]{2,1,0:T(1,128)S(1)} %get-tuple-element.88), channel_id=1, source_target_pairs={{0,1},{1,2},{2,3},{3,4},{4,5},{5,6},{6,7},{7,8},{8,9},{9,10},{10,1... | collective-permute-start | bytes 786440 | tf_op jit(solution)/shard_map/ppermute | solution.py:20
  8.0 0.7 slice_bitcast_fusion.5
  8.7 2.8 %collective-permute-start.2 = (f32[4,512]{1,0:T(4,128)S(1)}, f32[4,512]{1,0:T(4,128)S(1)}, u32[]{:S(2)}, u32[]{:S(2)}) collective-permute-start(f32[4,512]{1,0:T(4,128)S(1)} %slice_bitcast_fusion.5), channel_id=1, source_target_pairs={{16,0},{17,1},{18,2},{19,3},{20,4},{21,5},{22,6},{23,7},{24,8},{25... | collective-permute-start | bytes 24584 | tf_op jit(solution)/shard_map/ppermute | solution.py:12
  12.2 1.2 slice.310
  14.1 5.5 %collective-permute-done.1 = f32[128,1,512]{2,1,0:T(1,128)S(1)} collective-permute-done((f32[128,1,512]{2,1,0:T(1,128)S(1)}, f32[128,1,512]{2,1,0:T(1,128)S(1)}, u32[]{:S(2)}, u32[]{:S(2)}) %collective-permute-start.1) | collective-permute-done | bytes 262176 | tf_op jit(solution)/shard_map/ppermute | solution.py:20
  19.5 3.9 %fusion.3 = f32[128,4,512]{2,1,0:T(4,128)S(1)} fusion(f32[128,4,512]{2,1,0:T(4,128)S(1)} %copy-done, f32[128,4,512]{2,1,0:T(4,128)} %param.17, f32[128,1,512]{2,1,0:T(1,128)S(1)} %collective-permute-done.1, f32[128,1,512]{2,1,0:T(1,128)S(1)} %collective-permute-done, f32[128]{0:T(128)S(1)} %copy-done.2), kind=kLoop, calls=%fused_computation.15 | loop fusion | flops 1835008 | bytes 3670528 | tf_op jit(solution)/shard_map/add | solution.py:55
  24.3 1.8 %fusion.48 = f32[2048,128]{1,0:T(8,128)S(1)} fusion(f32[128,2048]{1,0:T(8,128)S(1)} %bitcast.93, f32[128,128]{1,0:T(8,128)S(1)} %copy-done.1), kind=kOutput, calls=%fused_computation.97 | convolution fusion | flops 402653184 | bytes 2162688 | tf_op jit(solution)/shard_map/dot_general | solution.py:31
  26.1 0.6 fusion.34
  26.8 1.3 collective-permute-start.3
  28.2 0.5 copy.12
  28.7 1.2 collective-permute-done.3
  30.5 1.3 collective-permute-start.4
  31.8 4.7 %collective-permute-start.5 = (f32[128,1,512]{2,1,0:T(1,128)S(1)}, f32[128,1,512]{2,1,0:T(1,128)S(1)}, u32[]{:S(2)}, u32[]{:S(2)}) collective-permute-start(f32[128,1,512]{2,1,0:T(1,128)S(1)} %get-tuple-element.86), channel_id=1, source_target_pairs={{0,1},{1,2},{2,3},{3,4},{4,5},{5,6},{6,7},{7,8},{8,9},{9,10},{10,1... | collective-permute-start | bytes 786440 | tf_op jit(solution)/shard_map/ppermute | solution.py:20
  36.6 2.4 %collective-permute-start.6 = (f32[4,512]{1,0:T(4,128)S(1)}, f32[4,512]{1,0:T(4,128)S(1)}, u32[]{:S(2)}, u32[]{:S(2)}) collective-permute-start(f32[4,512]{1,0:T(4,128)S(1)} %slice_bitcast_fusion.4), channel_id=1, source_target_pairs={{16,0},{17,1},{18,2},{19,3},{20,4},{21,5},{22,6},{23,7},{24,8},{25... | collective-permute-start | bytes 24584 | tf_op jit(solution)/shard_map/ppermute | solution.py:12
  39.0 2.2 %collective-permute-done.4 = f32[128,1,512]{2,1,0:T(1,128)S(1)} collective-permute-done((f32[128,1,512]{2,1,0:T(1,128)S(1)}, f32[128,1,512]{2,1,0:T(1,128)S(1)}, u32[]{:S(2)}, u32[]{:S(2)}) %collective-permute-start.4) | collective-permute-done | bytes 262176 | tf_op jit(solution)/shard_map/ppermute | solution.py:23
  41.1 4.5 %collective-permute-done.5 = f32[128,1,512]{2,1,0:T(1,128)S(1)} collective-permute-done((f32[128,1,512]{2,1,0:T(1,128)S(1)}, f32[128,1,512]{2,1,0:T(1,128)S(1)}, u32[]{:S(2)}, u32[]{:S(2)}) %collective-permute-start.5) | collective-permute-done | bytes 262176 | tf_op jit(solution)/shard_map/ppermute | solution.py:20
  45.6 1.7 %fusion.7 = f32[128,4,512]{2,1,0:T(4,128)S(1)} fusion(f32[128,4,512]{2,1,0:T(4,128)S(1)} %copy-done, f32[128,4,512]{2,1,0:T(4,128)S(1)} %multiply_add_fusion.5, f32[128,1,512]{2,1,0:T(1,128)S(1)} %collective-permute-done.5, f32[128,1,512]{2,1,0:T(1,128)S(1)} %collective-permute-done.4, f32[128]{0:T(128)S(1)} %copy-done.2), kind=kLoop, calls=%fused_computation.19 | loop fusion | flops 1835008 | bytes 3670528 | tf_op jit(solution)/shard_map/add | solution.py:55
  47.7 1.8 %fusion.49 = f32[2048,128]{1,0:T(8,128)S(1)} fusion(f32[128,2048]{1,0:T(8,128)S(1)} %bitcast.94, f32[128,128]{1,0:T(8,128)S(1)} %copy-done.1), kind=kOutput, calls=%fused_computation.98 | convolution fusion | flops 402653184 | bytes 2162688 | tf_op jit(solution)/shard_map/dot_general | solution.py:31
  49.5 0.6 fusion.32
  50.2 1.3 collective-permute-start.7
  52.0 1.3 collective-permute-done.7
  53.9 1.3 collective-permute-start.8
  55.2 4.7 %collective-permute-start.9 = (f32[128,1,512]{2,1,0:T(1,128)S(1)}, f32[128,1,512]{2,1,0:T(1,128)S(1)}, u32[]{:S(2)}, u32[]{:S(2)}) collective-permute-start(f32[128,1,512]{2,1,0:T(1,128)S(1)} %get-tuple-element.84), channel_id=1, source_target_pairs={{0,1},{1,2},{2,3},{3,4},{4,5},{5,6},{6,7},{7,8},{8,9},{9,10},{10,1... | collective-permute-start | bytes 786440 | tf_op jit(solution)/shard_map/ppermute | solution.py:20
  60.0 2.5 %collective-permute-start.10 = (f32[4,512]{1,0:T(4,128)S(1)}, f32[4,512]{1,0:T(4,128)S(1)}, u32[]{:S(2)}, u32[]{:S(2)}) collective-permute-start(f32[4,512]{1,0:T(4,128)S(1)} %slice_bitcast_fusion.3), channel_id=1, source_target_pairs={{16,0},{17,1},{18,2},{19,3},{20,4},{21,5},{22,6},{23,7},{24,8},{25... | collective-permute-start | bytes 24584 | tf_op jit(solution)/shard_map/ppermute | solution.py:12
  62.5 2.0 %collective-permute-done.8 = f32[128,1,512]{2,1,0:T(1,128)S(1)} collective-permute-done((f32[128,1,512]{2,1,0:T(1,128)S(1)}, f32[128,1,512]{2,1,0:T(1,128)S(1)}, u32[]{:S(2)}, u32[]{:S(2)}) %collective-permute-start.8) | collective-permute-done | bytes 262176 | tf_op jit(solution)/shard_map/ppermute | solution.py:23
  64.5 7.1 %collective-permute-done.9 = f32[128,1,512]{2,1,0:T(1,128)S(1)} collective-permute-done((f32[128,1,512]{2,1,0:T(1,128)S(1)}, f32[128,1,512]{2,1,0:T(1,128)S(1)}, u32[]{:S(2)}, u32[]{:S(2)}) %collective-permute-start.9) | collective-permute-done | bytes 262176 | tf_op jit(solution)/shard_map/ppermute | solution.py:20
  71.6 1.7 %fusion.11 = f32[128,4,512]{2,1,0:T(4,128)S(1)} fusion(f32[128,4,512]{2,1,0:T(4,128)S(1)} %copy-done, f32[128,4,512]{2,1,0:T(4,128)S(1)} %multiply_add_fusion.4, f32[128,1,512]{2,1,0:T(1,128)S(1)} %collective-permute-done.9, f32[128,1,512]{2,1,0:T(1,128)S(1)} %collective-permute-done.8, f32[128]{0:T(128)S(1)} %copy-done.2), kind=kLoop, calls=%fused_computation.23 | loop fusion | flops 1835008 | bytes 3670528 | tf_op jit(solution)/shard_map/add | solution.py:55
  73.7 1.8 %fusion.50 = f32[2048,128]{1,0:T(8,128)S(1)} fusion(f32[128,2048]{1,0:T(8,128)S(1)} %bitcast.95, f32[128,128]{1,0:T(8,128)S(1)} %copy-done.1), kind=kOutput, calls=%fused_computation.99 | convolution fusion | flops 402653184 | bytes 2162688 | tf_op jit(solution)/shard_map/dot_general | solution.py:31
  75.5 0.6 fusion.30
  76.2 1.3 collective-permute-start.11
  78.0 1.3 collective-permute-done.11
  79.9 1.3 collective-permute-start.12
  81.2 4.7 %collective-permute-start.13 = (f32[128,1,512]{2,1,0:T(1,128)S(1)}, f32[128,1,512]{2,1,0:T(1,128)S(1)}, u32[]{:S(2)}, u32[]{:S(2)}) collective-permute-start(f32[128,1,512]{2,1,0:T(1,128)S(1)} %get-tuple-element.82), channel_id=1, source_target_pairs={{0,1},{1,2},{2,3},{3,4},{4,5},{5,6},{6,7},{7,8},{8,9},{9,10},{10,1... | collective-permute-start | bytes 786440 | tf_op jit(solution)/shard_map/ppermute | solution.py:20
  86.0 2.4 %collective-permute-start.14 = (f32[4,512]{1,0:T(4,128)S(1)}, f32[4,512]{1,0:T(4,128)S(1)}, u32[]{:S(2)}, u32[]{:S(2)}) collective-permute-start(f32[4,512]{1,0:T(4,128)S(1)} %slice_bitcast_fusion.2), channel_id=1, source_target_pairs={{16,0},{17,1},{18,2},{19,3},{20,4},{21,5},{22,6},{23,7},{24,8},{25... | collective-permute-start | bytes 24584 | tf_op jit(solution)/shard_map/ppermute | solution.py:12
  88.3 2.2 %collective-permute-done.12 = f32[128,1,512]{2,1,0:T(1,128)S(1)} collective-permute-done((f32[128,1,512]{2,1,0:T(1,128)S(1)}, f32[128,1,512]{2,1,0:T(1,128)S(1)}, u32[]{:S(2)}, u32[]{:S(2)}) %collective-permute-start.12) | collective-permute-done | bytes 262176 | tf_op jit(solution)/shard_map/ppermute | solution.py:23
  90.5 4.5 %collective-permute-done.13 = f32[128,1,512]{2,1,0:T(1,128)S(1)} collective-permute-done((f32[128,1,512]{2,1,0:T(1,128)S(1)}, f32[128,1,512]{2,1,0:T(1,128)S(1)}, u32[]{:S(2)}, u32[]{:S(2)}) %collective-permute-start.13) | collective-permute-done | bytes 262176 | tf_op jit(solution)/shard_map/ppermute | solution.py:20
  95.0 1.7 %fusion.15 = f32[128,4,512]{2,1,0:T(4,128)S(1)} fusion(f32[128,4,512]{2,1,0:T(4,128)S(1)} %copy-done, f32[128,4,512]{2,1,0:T(4,128)S(1)} %multiply_add_fusion.3, f32[128,1,512]{2,1,0:T(1,128)S(1)} %collective-permute-done.13, f32[128,1,512]{2,1,0:T(1,128)S(1)} %collective-permute-done.12, f32[128]{0:T(128)S(1)} %copy-done.2), kind=kLoop, calls=%fused_computation.27 | loop fusion | flops 1835008 | bytes 3670528 | tf_op jit(solution)/shard_map/add | solution.py:55
  97.1 1.8 %fusion.51 = f32[2048,128]{1,0:T(8,128)S(1)} fusion(f32[128,2048]{1,0:T(8,128)S(1)} %bitcast.96, f32[128,128]{1,0:T(8,128)S(1)} %copy-done.1), kind=kOutput, calls=%fused_computation.100 | convolution fusion | flops 402653184 | bytes 2162688 | tf_op jit(solution)/shard_map/dot_general | solution.py:31
  98.9 0.6 fusion.28
  99.6 1.3 collective-permute-start.15
  101.4 1.3 collective-permute-done.15
  103.3 1.3 collective-permute-start.16
  104.6 4.7 %collective-permute-start.17 = (f32[128,1,512]{2,1,0:T(1,128)S(1)}, f32[128,1,512]{2,1,0:T(1,128)S(1)}, u32[]{:S(2)}, u32[]{:S(2)}) collective-permute-start(f32[128,1,512]{2,1,0:T(1,128)S(1)} %get-tuple-element.80), channel_id=1, source_target_pairs={{0,1},{1,2},{2,3},{3,4},{4,5},{5,6},{6,7},{7,8},{8,9},{9,10},{10,1... | collective-permute-start | bytes 786440 | tf_op jit(solution)/shard_map/ppermute | solution.py:20
  109.4 2.6 %collective-permute-start.18 = (f32[4,512]{1,0:T(4,128)S(1)}, f32[4,512]{1,0:T(4,128)S(1)}, u32[]{:S(2)}, u32[]{:S(2)}) collective-permute-start(f32[4,512]{1,0:T(4,128)S(1)} %slice_bitcast_fusion.1), channel_id=1, source_target_pairs={{16,0},{17,1},{18,2},{19,3},{20,4},{21,5},{22,6},{23,7},{24,8},{25... | collective-permute-start | bytes 24584 | tf_op jit(solution)/shard_map/ppermute | solution.py:12
  112.0 2.0 %collective-permute-done.16 = f32[128,1,512]{2,1,0:T(1,128)S(1)} collective-permute-done((f32[128,1,512]{2,1,0:T(1,128)S(1)}, f32[128,1,512]{2,1,0:T(1,128)S(1)}, u32[]{:S(2)}, u32[]{:S(2)}) %collective-permute-start.16) | collective-permute-done | bytes 262176 | tf_op jit(solution)/shard_map/ppermute | solution.py:23
  113.9 7.1 %collective-permute-done.17 = f32[128,1,512]{2,1,0:T(1,128)S(1)} collective-permute-done((f32[128,1,512]{2,1,0:T(1,128)S(1)}, f32[128,1,512]{2,1,0:T(1,128)S(1)}, u32[]{:S(2)}, u32[]{:S(2)}) %collective-permute-start.17) | collective-permute-done | bytes 262176 | tf_op jit(solution)/shard_map/ppermute | solution.py:20
  121.0 1.7 %fusion.19 = f32[128,4,512]{2,1,0:T(4,128)S(1)} fusion(f32[128,4,512]{2,1,0:T(4,128)S(1)} %copy-done, f32[128,4,512]{2,1,0:T(4,128)S(1)} %multiply_add_fusion.2, f32[128,1,512]{2,1,0:T(1,128)S(1)} %collective-permute-done.17, f32[128,1,512]{2,1,0:T(1,128)S(1)} %collective-permute-done.16, f32[128]{0:T(128)S(1)} %copy-done.2), kind=kLoop, calls=%fused_computation.31 | loop fusion | flops 1835008 | bytes 3670528 | tf_op jit(solution)/shard_map/add | solution.py:55
  123.1 1.8 %fusion.52 = f32[2048,128]{1,0:T(8,128)S(1)} fusion(f32[128,2048]{1,0:T(8,128)S(1)} %bitcast.97, f32[128,128]{1,0:T(8,128)S(1)} %copy-done.1), kind=kOutput, calls=%fused_computation.101 | convolution fusion | flops 402653184 | bytes 2162688 | tf_op jit(solution)/shard_map/dot_general | solution.py:31
  124.9 0.6 fusion.26
  125.6 1.3 collective-permute-start.19
  127.4 1.3 collective-permute-done.19
  129.3 1.3 collective-permute-start.20
  130.6 4.7 %collective-permute-start.21 = (f32[128,1,512]{2,1,0:T(1,128)S(1)}, f32[128,1,512]{2,1,0:T(1,128)S(1)}, u32[]{:S(2)}, u32[]{:S(2)}) collective-permute-start(f32[128,1,512]{2,1,0:T(1,128)S(1)} %get-tuple-element.78), channel_id=1, source_target_pairs={{0,1},{1,2},{2,3},{3,4},{4,5},{5,6},{6,7},{7,8},{8,9},{9,10},{10,1... | collective-permute-start | bytes 786440 | tf_op jit(solution)/shard_map/ppermute | solution.py:20
  135.4 2.4 %collective-permute-start.22 = (f32[4,512]{1,0:T(4,128)S(1)}, f32[4,512]{1,0:T(4,128)S(1)}, u32[]{:S(2)}, u32[]{:S(2)}) collective-permute-start(f32[4,512]{1,0:T(4,128)S(1)} %slice_bitcast_fusion), channel_id=1, source_target_pairs={{16,0},{17,1},{18,2},{19,3},{20,4},{21,5},{22,6},{23,7},{24,8},{25... | collective-permute-start | bytes 24584 | tf_op jit(solution)/shard_map/ppermute | solution.py:12
  137.7 2.2 %collective-permute-done.20 = f32[128,1,512]{2,1,0:T(1,128)S(1)} collective-permute-done((f32[128,1,512]{2,1,0:T(1,128)S(1)}, f32[128,1,512]{2,1,0:T(1,128)S(1)}, u32[]{:S(2)}, u32[]{:S(2)}) %collective-permute-start.20) | collective-permute-done | bytes 262176 | tf_op jit(solution)/shard_map/ppermute | solution.py:23
  139.9 4.5 %collective-permute-done.21 = f32[128,1,512]{2,1,0:T(1,128)S(1)} collective-permute-done((f32[128,1,512]{2,1,0:T(1,128)S(1)}, f32[128,1,512]{2,1,0:T(1,128)S(1)}, u32[]{:S(2)}, u32[]{:S(2)}) %collective-permute-start.21) | collective-permute-done | bytes 262176 | tf_op jit(solution)/shard_map/ppermute | solution.py:20
  144.4 1.7 %fusion.23 = f32[128,4,512]{2,1,0:T(4,128)S(1)} fusion(f32[128,4,512]{2,1,0:T(4,128)S(1)} %copy-done, f32[128,4,512]{2,1,0:T(4,128)S(1)} %multiply_add_fusion.1, f32[128,1,512]{2,1,0:T(1,128)S(1)} %collective-permute-done.21, f32[128,1,512]{2,1,0:T(1,128)S(1)} %collective-permute-done.20, f32[128]{0:T(128)S(1)} %copy-done.2), kind=kLoop, calls=%fused_computation.35 | loop fusion | flops 1835008 | bytes 3670528 | tf_op jit(solution)/shard_map/add | solution.py:55
  146.5 1.8 %fusion.53 = f32[2048,128]{1,0:T(8,128)S(1)} fusion(f32[128,2048]{1,0:T(8,128)S(1)} %bitcast.98, f32[128,128]{1,0:T(8,128)S(1)} %copy-done.1), kind=kOutput, calls=%fused_computation.102 | convolution fusion | flops 402653184 | bytes 2162688 | tf_op jit(solution)/shard_map/dot_general | solution.py:31
  148.3 0.6 fusion.24
  148.9 1.3 collective-permute-start.23
  150.7 1.3 collective-permute-done.23
  152.0 1.2 multiply_add_fusion
  (52 shorter events, 8.6 us)
Async XLA Ops:
  0.0 19.5 %copy-start = (f32[128,4,512]{2,1,0:T(4,128)S(1)}, f32[128,4,512]{2,1,0:T(4,128)}, u32[]{:S(2)}) copy-start(f32[128,4,512]{2,1,0:T(4,128)} %param.18) | copy-start | bytes 3145732
  0.0 19.5 %copy-start.2 = (f32[128]{0:T(128)S(1)}, f32[128]{0:T(128)}, u32[]{:S(2)}) copy-start(f32[128]{0:T(128)} %param.19) | copy-start | bytes 1540
  2.1 12.0 %collective-permute-start = (f32[128,1,512]{2,1,0:T(1,128)S(1)}, f32[128,1,512]{2,1,0:T(1,128)S(1)}, u32[]{:S(2)}, u32[]{:S(2)}) collective-permute-start(f32[128,1,512]{2,1,0:T(1,128)S(1)} %get-tuple-element.87), channel_id=1, source_target_pairs={{1,0},{2,1},{3,2},{4,3},{5,4},{6,5},{7,6},{8,7},{9,8},{10,9},{11,1... | collective-permute-start | bytes 786440 | tf_op jit(solution)/shard_map/ppermute | solution.py:23
  3.4 16.1 %collective-permute-start.1 = (f32[128,1,512]{2,1,0:T(1,128)S(1)}, f32[128,1,512]{2,1,0:T(1,128)S(1)}, u32[]{:S(2)}, u32[]{:S(2)}) collective-permute-start(f32[128,1,512]{2,1,0:T(1,128)S(1)} %get-tuple-element.88), channel_id=1, source_target_pairs={{0,1},{1,2},{2,3},{3,4},{4,5},{5,6},{6,7},{7,8},{8,9},{9,10},{10,1... | collective-permute-start | bytes 786440 | tf_op jit(solution)/shard_map/ppermute | solution.py:20
  8.7 14.8 %collective-permute-start.2 = (f32[4,512]{1,0:T(4,128)S(1)}, f32[4,512]{1,0:T(4,128)S(1)}, u32[]{:S(2)}, u32[]{:S(2)}) collective-permute-start(f32[4,512]{1,0:T(4,128)S(1)} %slice_bitcast_fusion.5), channel_id=1, source_target_pairs={{16,0},{17,1},{18,2},{19,3},{20,4},{21,5},{22,6},{23,7},{24,8},{25... | collective-permute-start | bytes 24584 | tf_op jit(solution)/shard_map/ppermute | solution.py:12
  23.5 0.8 copy-start.1
  26.8 3.1 %collective-permute-start.3 = (f32[4,512]{1,0:T(4,128)S(1)}, f32[4,512]{1,0:T(4,128)S(1)}, u32[]{:S(2)}, u32[]{:S(2)}) collective-permute-start(f32[4,512]{1,0:T(4,128)S(1)} %add.189), channel_id=1, source_target_pairs={{0,16},{1,17},{2,18},{3,19},{4,20},{5,21},{6,22},{7,23},{8,24},{9,... | collective-permute-start | bytes 24584 | tf_op jit(solution)/shard_map/ppermute | solution.py:12
  30.5 10.6 %collective-permute-start.4 = (f32[128,1,512]{2,1,0:T(1,128)S(1)}, f32[128,1,512]{2,1,0:T(1,128)S(1)}, u32[]{:S(2)}, u32[]{:S(2)}) collective-permute-start(f32[128,1,512]{2,1,0:T(1,128)S(1)} %get-tuple-element.85), channel_id=1, source_target_pairs={{1,0},{2,1},{3,2},{4,3},{5,4},{6,5},{7,6},{8,7},{9,8},{10,9},{11,1... | collective-permute-start | bytes 786440 | tf_op jit(solution)/shard_map/ppermute | solution.py:23
  31.8 13.8 %collective-permute-start.5 = (f32[128,1,512]{2,1,0:T(1,128)S(1)}, f32[128,1,512]{2,1,0:T(1,128)S(1)}, u32[]{:S(2)}, u32[]{:S(2)}) collective-permute-start(f32[128,1,512]{2,1,0:T(1,128)S(1)} %get-tuple-element.86), channel_id=1, source_target_pairs={{0,1},{1,2},{2,3},{3,4},{4,5},{5,6},{6,7},{7,8},{8,9},{9,10},{10,1... | collective-permute-start | bytes 786440 | tf_op jit(solution)/shard_map/ppermute | solution.py:20
  36.6 10.7 %collective-permute-start.6 = (f32[4,512]{1,0:T(4,128)S(1)}, f32[4,512]{1,0:T(4,128)S(1)}, u32[]{:S(2)}, u32[]{:S(2)}) collective-permute-start(f32[4,512]{1,0:T(4,128)S(1)} %slice_bitcast_fusion.4), channel_id=1, source_target_pairs={{16,0},{17,1},{18,2},{19,3},{20,4},{21,5},{22,6},{23,7},{24,8},{25... | collective-permute-start | bytes 24584 | tf_op jit(solution)/shard_map/ppermute | solution.py:12
  50.2 3.1 %collective-permute-start.7 = (f32[4,512]{1,0:T(4,128)S(1)}, f32[4,512]{1,0:T(4,128)S(1)}, u32[]{:S(2)}, u32[]{:S(2)}) collective-permute-start(f32[4,512]{1,0:T(4,128)S(1)} %add.197), channel_id=1, source_target_pairs={{0,16},{1,17},{2,18},{3,19},{4,20},{5,21},{6,22},{7,23},{8,24},{9,... | collective-permute-start | bytes 24584 | tf_op jit(solution)/shard_map/ppermute | solution.py:12
  53.9 10.6 %collective-permute-start.8 = (f32[128,1,512]{2,1,0:T(1,128)S(1)}, f32[128,1,512]{2,1,0:T(1,128)S(1)}, u32[]{:S(2)}, u32[]{:S(2)}) collective-permute-start(f32[128,1,512]{2,1,0:T(1,128)S(1)} %get-tuple-element.83), channel_id=1, source_target_pairs={{1,0},{2,1},{3,2},{4,3},{5,4},{6,5},{7,6},{8,7},{9,8},{10,9},{11,1... | collective-permute-start | bytes 786440 | tf_op jit(solution)/shard_map/ppermute | solution.py:23
  55.2 16.4 %collective-permute-start.9 = (f32[128,1,512]{2,1,0:T(1,128)S(1)}, f32[128,1,512]{2,1,0:T(1,128)S(1)}, u32[]{:S(2)}, u32[]{:S(2)}) collective-permute-start(f32[128,1,512]{2,1,0:T(1,128)S(1)} %get-tuple-element.84), channel_id=1, source_target_pairs={{0,1},{1,2},{2,3},{3,4},{4,5},{5,6},{6,7},{7,8},{8,9},{9,10},{10,1... | collective-permute-start | bytes 786440 | tf_op jit(solution)/shard_map/ppermute | solution.py:20
  60.0 13.4 %collective-permute-start.10 = (f32[4,512]{1,0:T(4,128)S(1)}, f32[4,512]{1,0:T(4,128)S(1)}, u32[]{:S(2)}, u32[]{:S(2)}) collective-permute-start(f32[4,512]{1,0:T(4,128)S(1)} %slice_bitcast_fusion.3), channel_id=1, source_target_pairs={{16,0},{17,1},{18,2},{19,3},{20,4},{21,5},{22,6},{23,7},{24,8},{25... | collective-permute-start | bytes 24584 | tf_op jit(solution)/shard_map/ppermute | solution.py:12
  76.2 3.1 %collective-permute-start.11 = (f32[4,512]{1,0:T(4,128)S(1)}, f32[4,512]{1,0:T(4,128)S(1)}, u32[]{:S(2)}, u32[]{:S(2)}) collective-permute-start(f32[4,512]{1,0:T(4,128)S(1)} %add.205), channel_id=1, source_target_pairs={{0,16},{1,17},{2,18},{3,19},{4,20},{5,21},{6,22},{7,23},{8,24},{9,... | collective-permute-start | bytes 24584 | tf_op jit(solution)/shard_map/ppermute | solution.py:12
  79.9 10.6 %collective-permute-start.12 = (f32[128,1,512]{2,1,0:T(1,128)S(1)}, f32[128,1,512]{2,1,0:T(1,128)S(1)}, u32[]{:S(2)}, u32[]{:S(2)}) collective-permute-start(f32[128,1,512]{2,1,0:T(1,128)S(1)} %get-tuple-element.81), channel_id=1, source_target_pairs={{1,0},{2,1},{3,2},{4,3},{5,4},{6,5},{7,6},{8,7},{9,8},{10,9},{11,1... | collective-permute-start | bytes 786440 | tf_op jit(solution)/shard_map/ppermute | solution.py:23
  81.2 13.8 %collective-permute-start.13 = (f32[128,1,512]{2,1,0:T(1,128)S(1)}, f32[128,1,512]{2,1,0:T(1,128)S(1)}, u32[]{:S(2)}, u32[]{:S(2)}) collective-permute-start(f32[128,1,512]{2,1,0:T(1,128)S(1)} %get-tuple-element.82), channel_id=1, source_target_pairs={{0,1},{1,2},{2,3},{3,4},{4,5},{5,6},{6,7},{7,8},{8,9},{9,10},{10,1... | collective-permute-start | bytes 786440 | tf_op jit(solution)/shard_map/ppermute | solution.py:20
  86.0 10.7 %collective-permute-start.14 = (f32[4,512]{1,0:T(4,128)S(1)}, f32[4,512]{1,0:T(4,128)S(1)}, u32[]{:S(2)}, u32[]{:S(2)}) collective-permute-start(f32[4,512]{1,0:T(4,128)S(1)} %slice_bitcast_fusion.2), channel_id=1, source_target_pairs={{16,0},{17,1},{18,2},{19,3},{20,4},{21,5},{22,6},{23,7},{24,8},{25... | collective-permute-start | bytes 24584 | tf_op jit(solution)/shard_map/ppermute | solution.py:12
  99.6 3.1 %collective-permute-start.15 = (f32[4,512]{1,0:T(4,128)S(1)}, f32[4,512]{1,0:T(4,128)S(1)}, u32[]{:S(2)}, u32[]{:S(2)}) collective-permute-start(f32[4,512]{1,0:T(4,128)S(1)} %add.213), channel_id=1, source_target_pairs={{0,16},{1,17},{2,18},{3,19},{4,20},{5,21},{6,22},{7,23},{8,24},{9,... | collective-permute-start | bytes 24584 | tf_op jit(solution)/shard_map/ppermute | solution.py:12
  103.3 10.6 %collective-permute-start.16 = (f32[128,1,512]{2,1,0:T(1,128)S(1)}, f32[128,1,512]{2,1,0:T(1,128)S(1)}, u32[]{:S(2)}, u32[]{:S(2)}) collective-permute-start(f32[128,1,512]{2,1,0:T(1,128)S(1)} %get-tuple-element.79), channel_id=1, source_target_pairs={{1,0},{2,1},{3,2},{4,3},{5,4},{6,5},{7,6},{8,7},{9,8},{10,9},{11,1... | collective-permute-start | bytes 786440 | tf_op jit(solution)/shard_map/ppermute | solution.py:23
  104.6 16.4 %collective-permute-start.17 = (f32[128,1,512]{2,1,0:T(1,128)S(1)}, f32[128,1,512]{2,1,0:T(1,128)S(1)}, u32[]{:S(2)}, u32[]{:S(2)}) collective-permute-start(f32[128,1,512]{2,1,0:T(1,128)S(1)} %get-tuple-element.80), channel_id=1, source_target_pairs={{0,1},{1,2},{2,3},{3,4},{4,5},{5,6},{6,7},{7,8},{8,9},{9,10},{10,1... | collective-permute-start | bytes 786440 | tf_op jit(solution)/shard_map/ppermute | solution.py:20
  109.4 13.4 %collective-permute-start.18 = (f32[4,512]{1,0:T(4,128)S(1)}, f32[4,512]{1,0:T(4,128)S(1)}, u32[]{:S(2)}, u32[]{:S(2)}) collective-permute-start(f32[4,512]{1,0:T(4,128)S(1)} %slice_bitcast_fusion.1), channel_id=1, source_target_pairs={{16,0},{17,1},{18,2},{19,3},{20,4},{21,5},{22,6},{23,7},{24,8},{25... | collective-permute-start | bytes 24584 | tf_op jit(solution)/shard_map/ppermute | solution.py:12
  125.6 3.1 %collective-permute-start.19 = (f32[4,512]{1,0:T(4,128)S(1)}, f32[4,512]{1,0:T(4,128)S(1)}, u32[]{:S(2)}, u32[]{:S(2)}) collective-permute-start(f32[4,512]{1,0:T(4,128)S(1)} %add.221), channel_id=1, source_target_pairs={{0,16},{1,17},{2,18},{3,19},{4,20},{5,21},{6,22},{7,23},{8,24},{9,... | collective-permute-start | bytes 24584 | tf_op jit(solution)/shard_map/ppermute | solution.py:12
  129.3 10.6 %collective-permute-start.20 = (f32[128,1,512]{2,1,0:T(1,128)S(1)}, f32[128,1,512]{2,1,0:T(1,128)S(1)}, u32[]{:S(2)}, u32[]{:S(2)}) collective-permute-start(f32[128,1,512]{2,1,0:T(1,128)S(1)} %get-tuple-element.77), channel_id=1, source_target_pairs={{1,0},{2,1},{3,2},{4,3},{5,4},{6,5},{7,6},{8,7},{9,8},{10,9},{11,1... | collective-permute-start | bytes 786440 | tf_op jit(solution)/shard_map/ppermute | solution.py:23
  130.6 13.8 %collective-permute-start.21 = (f32[128,1,512]{2,1,0:T(1,128)S(1)}, f32[128,1,512]{2,1,0:T(1,128)S(1)}, u32[]{:S(2)}, u32[]{:S(2)}) collective-permute-start(f32[128,1,512]{2,1,0:T(1,128)S(1)} %get-tuple-element.78), channel_id=1, source_target_pairs={{0,1},{1,2},{2,3},{3,4},{4,5},{5,6},{6,7},{7,8},{8,9},{9,10},{10,1... | collective-permute-start | bytes 786440 | tf_op jit(solution)/shard_map/ppermute | solution.py:20
  135.4 10.7 %collective-permute-start.22 = (f32[4,512]{1,0:T(4,128)S(1)}, f32[4,512]{1,0:T(4,128)S(1)}, u32[]{:S(2)}, u32[]{:S(2)}) collective-permute-start(f32[4,512]{1,0:T(4,128)S(1)} %slice_bitcast_fusion), channel_id=1, source_target_pairs={{16,0},{17,1},{18,2},{19,3},{20,4},{21,5},{22,6},{23,7},{24,8},{25... | collective-permute-start | bytes 24584 | tf_op jit(solution)/shard_map/ppermute | solution.py:12
  148.9 3.1 %collective-permute-start.23 = (f32[4,512]{1,0:T(4,128)S(1)}, f32[4,512]{1,0:T(4,128)S(1)}, u32[]{:S(2)}, u32[]{:S(2)}) collective-permute-start(f32[4,512]{1,0:T(4,128)S(1)} %add.229), channel_id=1, source_target_pairs={{0,16},{1,17},{2,18},{3,19},{4,20},{5,21},{6,22},{7,23},{8,24},{9,... | collective-permute-start | bytes 24584 | tf_op jit(solution)/shard_map/ppermute | solution.py:12
where the time goes:
time: 154 us; the launch traced here: 153 us
  starting transfers between devices  58.8 us (38%)
  waiting for transfers between devices  51.1 us (33%)
  other arithmetic  19 us (12%)
  local copies, waits for them, and re-layouts  11.6 us (8%)
  matrix products  10.8 us (7%)
  between operations  1.93 us (1%)
    ppermute x6, waiting for transfers between devices, extended(): lax.ppermute(lax.slice_in_dim(block, block.shape[dim] - width, None, axis...  33 us
    ppermute x6, starting transfers between devices, extended(): lax.ppermute(lax.slice_in_dim(block, block.shape[dim] - width, None, axis...  28.3 us
    ppermute x12, starting transfers between devices, shifted(): lax.ppermute(value, axis, [(source, source + steps) for source in range(f...  22.8 us
    add x6, other arithmetic, local(): right_side = source + weights * (across_rows + across_columns(field))  12.5 us
    dot_general x6, matrix products, apply_inverse(): jnp.dot(inverse, flat, precision=lax.Precision.HIGHEST, preferred_element...  10.8 us
    ppermute x6, waiting for transfers between devices, extended(): lax.ppermute(lax.slice_in_dim(block, 0, width, axis=dim), axis, backward)  10.6 us
    ppermute x6, starting transfers between devices, extended(): lax.ppermute(lax.slice_in_dim(block, 0, width, axis=dim), axis, backward)  7.75 us
    ppermute x12, waiting for transfers between devices, shifted(): lax.ppermute(value, axis, [(source, source + steps) for source in range(f...  7.5 us
  transfers between devices with their start and end apart: 24, of which 17 were waited for; matrix products, arithmetic and copies ran while one was open for 11% of the time, Pallas kernels for 0%

commit v1 on v0

v1 whole, which is shorter than its diff:
```python
import functools

import jax
import jax.numpy as jnp
from jax import lax
from jax.experimental import pallas as pl
from jax.experimental.pallas import tpu as pltpu
from jax.sharding import PartitionSpec as P

SWEEPS = 6
LANES = 128
MESH = pl.DeviceIdType.MESH
F32, BF16 = jnp.float32, jnp.bfloat16


def halves(value):
    high = value.astype(BF16)
    return high, (value - high.astype(F32)).astype(BF16)


def kernel(lat_count, temp, source, couple, face, inverse, out, field, src, above_below, sides, layer,
           side_out, layer_out, weights, matrix, local_sem, in_send, in_recv, row_send, row_recv,
           side_send, side_recv, layer_send, layer_recv, out_send, out_recv):
    tile_rows, depth, cols = temp.shape
    group = cols // LANES
    rows = tile_rows * group
    blocks = depth // rows
    k = lax.axis_index("depth")
    me = lax.axis_index("lat")
    q = lax.rem(me, group)
    base = me - q
    has_up, has_down = base > 0, base + group < lat_count
    has_left, has_right = q > 0, q < group - 1

    above_below[...] = jnp.zeros_like(above_below)
    sides[...] = jnp.zeros_like(sides)

    barrier = pltpu.get_barrier_semaphore()

    def greet(device):
        pl.semaphore_signal(barrier, inc=1, device_id=device, device_id_type=MESH)

    greet((1 - k, me))
    for offset in range(1, group):
        greet((k, base + lax.rem(q + offset, group)))
    pl.when(has_up)(lambda: greet((k, me - group)))
    pl.when(has_down)(lambda: greet((k, me + group)))
    pl.semaphore_wait(barrier, group + has_up.astype(jnp.int32) + has_down.astype(jnp.int32))

    def columns(index):
        return pl.ds(pl.multiple_of(index * LANES, LANES), LANES)

    def remote(src_ref, dst_ref, send, recv, device):
        return pltpu.make_async_remote_copy(
            src_ref=src_ref, dst_ref=dst_ref, send_sem=send, recv_sem=recv, device_id=device, device_id_type=MESH
        )

    def incoming(which, given, landing, offset):
        partner = lax.rem(q + offset, group)
        return remote(
            given.at[:, :, columns(partner)], landing.at[pl.ds(q * tile_rows, tile_rows)],
            in_send.at[which, offset], in_recv.at[which, offset], (k, base + partner),
        )

    pairs = ((temp, field.at[0]), (source, src))
    own = []
    for which, (given, landing) in enumerate(pairs):
        for offset in range(1, group):
            incoming(which, given, landing, offset).start()
        own.append(pltpu.make_async_copy(
            given.at[:, :, columns(q)], landing.at[pl.ds(q * tile_rows, tile_rows)], local_sem.at[which]
        ))
        own[-1].start()

    high, low = halves(inverse[...])
    matrix[:depth, :depth] = high
    matrix[:depth, depth:] = high
    matrix[depth:, :depth] = low
    matrix[depth:, depth:] = jnp.zeros_like(low)
    weights[...] = jnp.transpose(jnp.broadcast_to(couple[...], (LANES, depth)))

    lane = lax.broadcasted_iota(jnp.int32, (rows, LANES), 1)
    first_lane = lax.broadcasted_iota(jnp.int32, (depth, LANES), 1) == 0
    last_lane = lax.broadcasted_iota(jnp.int32, (depth, LANES), 1) == LANES - 1
    edge_layer = jnp.where(k == 0, depth - 1, 0)
    face_gain = jnp.where(lax.broadcasted_iota(jnp.int32, (depth, LANES), 0) == edge_layer, face[0], 0.0)

    def row_copy(slot, parity):
        if slot == 0:
            return remote(field.at[parity, rows - 1], above_below.at[parity, 0], row_send.at[parity, 0],
                          row_recv.at[parity, 0], (k, me + group))
        return remote(field.at[parity, 0], above_below.at[parity, 1], row_send.at[parity, 1],
                      row_recv.at[parity, 1], (k, me - group))

    def side_copy(slot, parity):
        return remote(side_out.at[slot], sides.at[parity, slot], side_send.at[parity, slot],
                      side_recv.at[parity, slot], (k, me + 1 if slot == 0 else me - 1))

    def layer_copy():
        return remote(layer_out, layer, layer_send, layer_recv, (1 - k, me))

    goes = (has_down, has_up)
    comes = (has_up, has_down)
    side_goes = (has_right, has_left)
    side_comes = (has_left, has_right)

    def start_rows(parity):
        for slot in range(2):
            pl.when(goes[slot])(lambda slot=slot: row_copy(slot, parity).start())

    def start_sides(parity):
        for slot in range(2):
            pl.when(side_goes[slot])(lambda slot=slot: side_copy(slot, parity).start())

    def finish_halo(parity):
        for slot in range(2):
            pl.when(comes[slot])(lambda slot=slot: row_copy(slot, parity).wait_recv())
            pl.when(goes[slot])(lambda slot=slot: row_copy(slot, parity).wait_send())
            pl.when(side_comes[slot])(lambda slot=slot: side_copy(slot, parity).wait_recv())
            pl.when(side_goes[slot])(lambda slot=slot: side_copy(slot, parity).wait_send())

    def pack(row, value, packed):
        right, left = packed
        for block in range(blocks):
            place = block * rows + row
            part = value[block * rows:(block + 1) * rows]
            at = lane == place
            right = jnp.where(at, pltpu.roll(part, (place + 1) % LANES, 1), right)
            left = jnp.where(at, pltpu.roll(part, place, 1) if place else part, left)
        return right, left

    def unpack(slot_value, row, lane_at):
        parts = []
        for block in range(blocks):
            shift = (lane_at - block * rows - row) % LANES
            parts.append(pltpu.roll(slot_value, shift, 1) if shift else slot_value)
        return jnp.concatenate(parts, axis=0)

    def keep_layer(row, value):
        layer_out[row:row + 1, :] = jnp.where(k == 0, value[depth - 1:depth], value[0:1])

    nothing = (jnp.zeros((rows, LANES), F32), jnp.zeros((rows, LANES), F32))

    own[0].wait()
    for offset in range(1, group):
        incoming(0, temp, field.at[0], offset).wait()
    start_rows(0)
    packed = nothing
    for row in range(rows):
        value = field[0, row]
        packed = pack(row, value, packed)
        keep_layer(row, value)
    side_out[0], side_out[1] = packed
    start_sides(0)
    pl.when(k == 1)(lambda: layer_copy().start())
    own[1].wait()
    for offset in range(1, group):
        incoming(1, source, src, offset).wait()

    order = [(0, rows - 1)] + [(row, row + 1) for row in range(1, rows - 1, 2)]

    def sweep(step, carry):
        parity = lax.rem(step, 2)
        later = 1 - parity
        finish_halo(parity)
        pl.when((k == 1) | (step > 0))(lambda: layer_copy().wait_send())
        layer_copy().wait_recv()
        other = layer[...]
        from_left, from_right = sides[parity, 0], sides[parity, 1]
        packed = nothing
        for number, pair in enumerate(order):
            sums = []
            for row in pair:
                here = field[parity, row]
                up = field[parity, row - 1] if row > 0 else above_below[parity, 0]
                down = field[parity, row + 1] if row < rows - 1 else above_below[parity, 1]
                before = jnp.where(first_lane, unpack(from_left, row, 0), pltpu.roll(here, 1, 1))
                after = jnp.where(last_lane, unpack(from_right, row, LANES - 1), pltpu.roll(here, LANES - 1, 1))
                right_side = src[row] + weights[...] * ((up + down) + (before + after))
                sums.append(right_side + face_gain * other[row:row + 1])
            high, low = halves(jnp.concatenate(sums, axis=1))
            product = jnp.dot(matrix[...], jnp.concatenate([high, low], axis=0), preferred_element_type=F32)
            solved = product[:depth] + product[depth:]
            for at, row in enumerate(pair):
                value = solved[:, at * LANES:(at + 1) * LANES]
                field[later, row] = value
                packed = pack(row, value, packed)
                keep_layer(row, value)
            if number == 0:
                pl.when(step < SWEEPS - 1)(lambda: start_rows(later))
        pl.when((k == 0) | (step < SWEEPS - 1))(lambda: layer_copy().start())
        side_out[0], side_out[1] = packed
        pl.when(step < SWEEPS - 1)(lambda: start_sides(later))
        return carry

    lax.fori_loop(0, SWEEPS, sweep, 0)

    final = SWEEPS % 2

    def outgoing(offset):
        partner = lax.rem(q + offset, group)
        return remote(
            field.at[final, pl.ds(partner * tile_rows, tile_rows)], out.at[:, :, columns(q)],
            out_send.at[offset], out_recv.at[offset], (k, base + partner),
        )

    for offset in range(1, group):
        outgoing(offset).start()
    mine = pltpu.make_async_copy(
        field.at[final, pl.ds(q * tile_rows, tile_rows)], out.at[:, :, columns(q)], local_sem.at[0]
    )
    mine.start()
    pl.when(k == 0)(lambda: layer_copy().wait_send())
    for offset in range(1, group):
        outgoing(offset).wait()
    mine.wait()


def solution(mesh):
    lat_count = mesh.shape["lat"]

    def local(temp_old, source, lat_couple, face_couple, block_inverse):
        depth, tile_rows, cols = temp_old.shape
        group = cols // LANES
        rows = tile_rows * group
        vmem = pl.BlockSpec(memory_space=pltpu.VMEM)
        dma = pltpu.SemaphoreType.DMA
        result = pl.pallas_call(
            functools.partial(kernel, lat_count),
            out_shape=jax.ShapeDtypeStruct((tile_rows, depth, cols), F32),
            in_specs=[vmem, vmem, vmem, pl.BlockSpec(memory_space=pltpu.SMEM), vmem],
            out_specs=vmem,
            scratch_shapes=[
                pltpu.VMEM((2, rows, depth, LANES), F32),
                pltpu.VMEM((rows, depth, LANES), F32),
                pltpu.VMEM((2, 2, depth, LANES), F32),
                pltpu.VMEM((2, 2, rows, LANES), F32),
                pltpu.VMEM((rows, LANES), F32),
                pltpu.VMEM((2, rows, LANES), F32),
                pltpu.VMEM((rows, LANES), F32),
                pltpu.VMEM((depth, LANES), F32),
                pltpu.VMEM((2 * depth, 2 * depth), BF16),
                dma((2,)),
                dma((2, group)), dma((2, group)),
                dma((2, 2)), dma((2, 2)),
                dma((2, 2)), dma((2, 2)),
                dma, dma,
                dma((group,)), dma((group,)),
            ],
            compiler_params=pltpu.CompilerParams(collective_id=0, has_side_effects=True),
        )(
            jnp.transpose(temp_old, (1, 0, 2)), jnp.transpose(source, (1, 0, 2)),
            lat_couple.reshape(1, depth), face_couple, block_inverse,
        )
        return jnp.transpose(result, (1, 0, 2))

    return jax.shard_map(
        local,
        mesh=mesh,
        in_specs=(P("depth", "lat", None), P("depth", "lat", None), P("depth"), P(), P("depth", None)),
        out_specs=P("depth", "lat", None),
        check_vma=False,
    )
```

time: 154 us -> 88.6 us (0.58)
  Pallas kernels: 0 us -> 81.4 us
  starting transfers between devices: 58.8 us -> 0 us
  waiting for transfers between devices: 51.1 us -> 0 us
  other arithmetic: 19 us -> 0 us
  matrix products: 10.8 us -> 0 us
  local copies, waits for them, and re-layouts: 11.6 us -> 6.37 us
    pallas_call x0 -> x1, Pallas kernels: none -> 81.4 us  [local(): pl.pallas_call(functools.partial(kernel, lat_count), out_shape=jax.ShapeD...]
    ppermute x24 -> x0, starting transfers between devices: 58.8 us -> none  [the longest x6 28.3 us: extended(): lax.ppermute(lax.slice_in_dim(block, block.shape[dim] - width, None, axis...]
    ppermute x24 -> x0, waiting for transfers between devices: 51.1 us -> none  [the longest x6 33 us: extended(): lax.ppermute(lax.slice_in_dim(block, block.shape[dim] - width, None, axis...]
    add x18 -> x0, other arithmetic: 18.8 us -> none  [the longest x6 12.5 us: local(): right_side = source + weights * (across_rows + across_columns(field))]
    dot_general x6 -> x0, matrix products: 10.8 us -> none  [apply_inverse(): jnp.dot(inverse, flat, precision=lax.Precision.HIGHEST, preferred_element...]
    transpose x0 -> x2, local copies, waits for them, and re-layouts: none -> 6.37 us  [the longest x1 3.5 us: local(): jnp.transpose(source, (1, 0, 2))]
    slice x7 -> x0, local copies, waits for them, and re-layouts: 5.34 us -> none  [the longest x6 4.11 us: extended(): lax.slice_in_dim(block, 0, width, axis=dim)]
    reshape x6 -> x0, local copies, waits for them, and re-layouts: 2.95 us -> none  [apply_inverse(): return jnp.dot(inverse, flat, precision=lax.Precision.HIGHEST, preferred_...]
  transfers between devices with their start and end apart: 24 -> 0, of which waited for: 17 -> 0; matrix products, arithmetic and copies ran while one was open for 11% -> 0% of each run, Pallas kernels for 0% -> 0%
where the time goes in v1:
time: 88.6 us; the launch traced here: 88.4 us
  Pallas kernels  81.4 us (92%)
  local copies, waits for them, and re-layouts  6.37 us (7%)
    pallas_call x1, Pallas kernels, local(): pl.pallas_call(functools.partial(kernel, lat_count), out_shape=jax.ShapeD...  81.4 us
    transpose x1, local copies, waits for them, and re-layouts, local(): jnp.transpose(source, (1, 0, 2))  3.5 us
    transpose x1, local copies, waits for them, and re-layouts, local(): return jnp.transpose(result, (1, 0, 2))  2.87 us

profile of v1, /device:TPU:1, one launch (start us, length us, event | category | flops | bytes accessed | tf_op | source)
XLA Modules:
  0.0 88.4 jit_solution(644438032032950968)
XLA Ops:
  0.7 3.5 %copy_bitcast_fusion = (f32[4,128,512]{2,1,0:T(8,128)}, f32[4,128,512]{2,1,0:T(8,128)}) fusion(f32[128,4,512]{2,1,0:T(4,128)} %param.6, f32[128,4,512]{2,1,0:T(4,128)} %param.5), kind=kLoop, calls=%fused_computation | loop fusion | bytes 4194304 | tf_op jit(solution)/shard_map/transpose | solution.py:252
  4.1 81.4 %shard_map.55 = f32[4,128,512]{2,1,0:T(8,128)} custom-call(f32[4,128,512]{2,1,0:T(8,128)} %get-tuple-element.6.temp, f32[4,128,512]{2,1,0:T(8,128)} %get-tuple-element.5.source, f32[1,128]{1,0:T(1,128)} %bitcast.7, f32[1]{0:T(128)S(6)} %copy.11.face, f32[128,128]{1,0:T(8,128)} %inverse.1), custom_call_target="tpu_custom_call" | custom-call | tf_op jit(solution)/shard_map/pallas_call | solution.py:228
  85.5 2.9 %copy.8 = f32[128,4,512]{2,1,0:T(4,128)} copy(f32[128,4,512]{2,0,1:T(8,128)} %bitcast.6) | data formatting | bytes 2097152 | tf_op jit(solution)/shard_map/transpose | solution.py:255

commit v2 on v1

--- a/solution.py
+++ b/solution.py
@@ -9,6 +9,7 @@
 
 SWEEPS = 6
 LANES = 128
+SUBLANES = 8
 MESH = pl.DeviceIdType.MESH
 F32, BF16 = jnp.float32, jnp.bfloat16
 
@@ -24,7 +25,11 @@
     tile_rows, depth, cols = temp.shape
     group = cols // LANES
     rows = tile_rows * group
-    blocks = depth // rows
+    order = [(0, rows - 1)] + [(row, row + 1) for row in range(1, rows - 1, 2)]
+    turn = [row for pair in order for row in pair]
+    layer_rows, side_rows = layer.shape[0], sides.shape[2]
+    layer_rows, side_rows = rows // layer_rows, rows // side_rows
+    blocks = depth // SUBLANES
     k = lax.axis_index("depth")
     me = lax.axis_index("lat")
     q = lax.rem(me, group)
@@ -79,7 +84,7 @@
     matrix[depth:, depth:] = jnp.zeros_like(low)
     weights[...] = jnp.transpose(jnp.broadcast_to(couple[...], (LANES, depth)))
 
-    lane = lax.broadcasted_iota(jnp.int32, (rows, LANES), 1)
+    lane = lax.broadcasted_iota(jnp.int32, (SUBLANES, LANES), 1)
     first_lane = lax.broadcasted_iota(jnp.int32, (depth, LANES), 1) == 0
     last_lane = lax.broadcasted_iota(jnp.int32, (depth, LANES), 1) == LANES - 1
     edge_layer = jnp.where(k == 0, depth - 1, 0)
@@ -92,12 +97,12 @@
         return remote(field.at[parity, 0], above_below.at[parity, 1], row_send.at[parity, 1],
                       row_recv.at[parity, 1], (k, me - group))
 
-    def side_copy(slot, parity):
-        return remote(side_out.at[slot], sides.at[parity, slot], side_send.at[parity, slot],
-                      side_recv.at[parity, slot], (k, me + 1 if slot == 0 else me - 1))
-
-    def layer_copy():
-        return remote(layer_out, layer, layer_send, layer_recv, (1 - k, me))
+    def side_copy(slot, parity, chunk):
+        return remote(side_out.at[slot, chunk], sides.at[parity, slot, chunk], side_send.at[parity, slot, chunk],
+                      side_recv.at[parity, slot, chunk], (k, me + 1 if slot == 0 else me - 1))
+
+    def layer_copy(chunk):
+        return remote(layer_out.at[chunk], layer.at[chunk], layer_send.at[chunk], layer_recv.at[chunk], (1 - k, me))
 
     goes = (has_down, has_up)
     comes = (has_up, has_down)
@@ -108,89 +113,102 @@
         for slot in range(2):
             pl.when(goes[slot])(lambda slot=slot: row_copy(slot, parity).start())
 
-    def start_sides(parity):
-        for slot in range(2):
-            pl.when(side_goes[slot])(lambda slot=slot: side_copy(slot, parity).start())
-
-    def finish_halo(parity):
+    def start_sides(parity, chunk):
+        for slot in range(2):
+            pl.when(side_goes[slot])(lambda slot=slot: side_copy(slot, parity, chunk).start())
+
+    def finish_rows(parity):
         for slot in range(2):
             pl.when(comes[slot])(lambda slot=slot: row_copy(slot, parity).wait_recv())
             pl.when(goes[slot])(lambda slot=slot: row_copy(slot, parity).wait_send())
-            pl.when(side_comes[slot])(lambda slot=slot: side_copy(slot, parity).wait_recv())
-            pl.when(side_goes[slot])(lambda slot=slot: side_copy(slot, parity).wait_send())
-
-    def pack(row, value, packed):
+
+    def finish_sides(parity, chunk):
+        for slot in range(2):
+            pl.when(side_comes[slot])(lambda slot=slot: side_copy(slot, parity, chunk).wait_recv())
+            pl.when(side_goes[slot])(lambda slot=slot: side_copy(slot, parity, chunk).wait_send())
+
+    def pack(index, value, packed):
         right, left = packed
         for block in range(blocks):
-            place = block * rows + row
-            part = value[block * rows:(block + 1) * rows]
+            place = block * side_rows + index % side_rows
+            part = value[block * SUBLANES:(block + 1) * SUBLANES]
             at = lane == place
-            right = jnp.where(at, pltpu.roll(part, (place + 1) % LANES, 1), right)
+            right = jnp.where(at, pltpu.roll(part, (place + 1) % LANES, 1) if place < LANES - 1 else part, right)
             left = jnp.where(at, pltpu.roll(part, place, 1) if place else part, left)
         return right, left
 
-    def unpack(slot_value, row, lane_at):
+    def unpack(slot_value, index, lane_at):
         parts = []
         for block in range(blocks):
-            shift = (lane_at - block * rows - row) % LANES
+            shift = (lane_at - block * side_rows - index % side_rows) % LANES
             parts.append(pltpu.roll(slot_value, shift, 1) if shift else slot_value)
         return jnp.concatenate(parts, axis=0)
 
-    def keep_layer(row, value):
-        layer_out[row:row + 1, :] = jnp.where(k == 0, value[depth - 1:depth], value[0:1])
-
-    nothing = (jnp.zeros((rows, LANES), F32), jnp.zeros((rows, LANES), F32))
+    def keep_layer(index, value):
+        at = index % layer_rows
+        layer_out[index // layer_rows, at:at + 1, :] = jnp.where(k == 0, value[depth - 1:depth], value[0:1])
+
+    nothing = (jnp.zeros((SUBLANES, LANES), F32), jnp.zeros((SUBLANES, LANES), F32))
 
     own[0].wait()
     for offset in range(1, group):
         incoming(0, temp, field.at[0], offset).wait()
     start_rows(0)
-    packed = nothing
-    for row in range(rows):
+    for index, row in enumerate(turn):
         value = field[0, row]
-        packed = pack(row, value, packed)
-        keep_layer(row, value)
-    side_out[0], side_out[1] = packed
-    start_sides(0)
-    pl.when(k == 1)(lambda: layer_copy().start())
+        packed = pack(index, value, nothing if index % side_rows == 0 else packed)
+        keep_layer(index, value)
+        if (index + 1) % layer_rows == 0:
+            pl.when(k == 1)(lambda chunk=index // layer_rows: layer_copy(chunk).start())
+        if (index + 1) % side_rows == 0:
+            chunk = index // side_rows
+            side_out[0, chunk], side_out[1, chunk] = packed
+            start_sides(0, chunk)
     own[1].wait()
     for offset in range(1, group):
         incoming(1, source, src, offset).wait()
-
-    order = [(0, rows - 1)] + [(row, row + 1) for row in range(1, rows - 1, 2)]
 
     def sweep(step, carry):
         parity = lax.rem(step, 2)
         later = 1 - parity
-        finish_halo(parity)
-        pl.when((k == 1) | (step > 0))(lambda: layer_copy().wait_send())
-        layer_copy().wait_recv()
-        other = layer[...]
-        from_left, from_right = sides[parity, 0], sides[parity, 1]
-        packed = nothing
+        finish_rows(parity)
         for number, pair in enumerate(order):
+            first = number * 2
+            chunk = first // side_rows
+            if first % side_rows == 0:
+                finish_sides(parity, chunk)
+                packed = nothing
+                from_left, from_right = sides[parity, 0, chunk], sides[parity, 1, chunk]
+            group_of = first // layer_rows
+            if first % layer_rows == 0:
+                pl.when((k == 1) | (step > 0))(lambda group_of=group_of: layer_copy(group_of).wait_send())
+                layer_copy(group_of).wait_recv()
+                other = layer[group_of]
             sums = []
-            for row in pair:
+            for index, row in enumerate(pair, first):
                 here = field[parity, row]
                 up = field[parity, row - 1] if row > 0 else above_below[parity, 0]
                 down = field[parity, row + 1] if row < rows - 1 else above_below[parity, 1]
-                before = jnp.where(first_lane, unpack(from_left, row, 0), pltpu.roll(here, 1, 1))
-                after = jnp.where(last_lane, unpack(from_right, row, LANES - 1), pltpu.roll(here, LANES - 1, 1))
+                before = jnp.where(first_lane, unpack(from_left, index, 0), pltpu.roll(here, 1, 1))
+                after = jnp.where(last_lane, unpack(from_right, index, LANES - 1), pltpu.roll(here, LANES - 1, 1))
                 right_side = src[row] + weights[...] * ((up + down) + (before + after))
-                sums.append(right_side + face_gain * other[row:row + 1])
+                at = index % layer_rows
+                sums.append(right_side + face_gain * other[at:at + 1])
             high, low = halves(jnp.concatenate(sums, axis=1))
             product = jnp.dot(matrix[...], jnp.concatenate([high, low], axis=0), preferred_element_type=F32)
             solved = product[:depth] + product[depth:]
             for at, row in enumerate(pair):
                 value = solved[:, at * LANES:(at + 1) * LANES]
                 field[later, row] = value
-                packed = pack(row, value, packed)
-                keep_layer(row, value)
+                packed = pack(first + at, value, packed)
+                keep_layer(first + at, value)
             if number == 0:
                 pl.when(step < SWEEPS - 1)(lambda: start_rows(later))
-        pl.when((k == 0) | (step < SWEEPS - 1))(lambda: layer_copy().start())
-        side_out[0], side_out[1] = packed
-        pl.when(step < SWEEPS - 1)(lambda: start_sides(later))
+            if (first + 2) % layer_rows == 0:
+                pl.when((k == 0) | (step < SWEEPS - 1))(lambda group_of=group_of: layer_copy(group_of).start())
+            if (first + 2) % side_rows == 0:
+                side_out[0, chunk], side_out[1, chunk] = packed
+                pl.when(step < SWEEPS - 1)(lambda chunk=chunk: start_sides(later, chunk))
         return carry
 
     lax.fori_loop(0, SWEEPS, sweep, 0)
@@ -210,7 +228,8 @@
         field.at[final, pl.ds(q * tile_rows, tile_rows)], out.at[:, :, columns(q)], local_sem.at[0]
     )
     mine.start()
-    pl.when(k == 0)(lambda: layer_copy().wait_send())
+    for chunk in range(layer.shape[0]):
+        pl.when(k == 0)(lambda chunk=chunk: layer_copy(chunk).wait_send())
     for offset in range(1, group):
         outgoing(offset).wait()
     mine.wait()
@@ -223,6 +242,8 @@
         depth, tile_rows, cols = temp_old.shape
         group = cols // LANES
         rows = tile_rows * group
+        side_chunks = rows * depth // (SUBLANES * LANES)
+        layer_chunks = rows // 4
         vmem = pl.BlockSpec(memory_space=pltpu.VMEM)
         dma = pltpu.SemaphoreType.DMA
         result = pl.pallas_call(
@@ -234,17 +255,17 @@
                 pltpu.VMEM((2, rows, depth, LANES), F32),
                 pltpu.VMEM((rows, depth, LANES), F32),
                 pltpu.VMEM((2, 2, depth, LANES), F32),
-                pltpu.VMEM((2, 2, rows, LANES), F32),
-                pltpu.VMEM((rows, LANES), F32),
-                pltpu.VMEM((2, rows, LANES), F32),
-                pltpu.VMEM((rows, LANES), F32),
+                pltpu.VMEM((2, 2, side_chunks, SUBLANES, LANES), F32),
+                pltpu.VMEM((layer_chunks, SUBLANES, LANES), F32),
+                pltpu.VMEM((2, side_chunks, SUBLANES, LANES), F32),
+                pltpu.VMEM((layer_chunks, SUBLANES, LANES), F32),
                 pltpu.VMEM((depth, LANES), F32),
                 pltpu.VMEM((2 * depth, 2 * depth), BF16),
                 dma((2,)),
                 dma((2, group)), dma((2, group)),
                 dma((2, 2)), dma((2, 2)),
-                dma((2, 2)), dma((2, 2)),
-                dma, dma,
+                dma((2, 2, side_chunks)), dma((2, 2, side_chunks)),
+                dma((layer_chunks,)), dma((layer_chunks,)),
                 dma((group,)), dma((group,)),
             ],
             compiler_params=pltpu.CompilerParams(collective_id=0, has_side_effects=True),

time: 88.6 us -> 79 us (0.89)
  Pallas kernels: 81.4 us -> 71.4 us
    pallas_call x1, Pallas kernels: 81.4 us -> 71.4 us  [local(): pl.pallas_call(functools.partial(kernel, lat_count), out_shape=jax.ShapeD...]
where the time goes in v2:
time: 79 us; the launch traced here: 78.5 us
  Pallas kernels  71.4 us (90%)
  local copies, waits for them, and re-layouts  6.37 us (8%)
    pallas_call x1, Pallas kernels, local(): pl.pallas_call(functools.partial(kernel, lat_count), out_shape=jax.ShapeD...  71.4 us
    transpose x1, local copies, waits for them, and re-layouts, local(): jnp.transpose(source, (1, 0, 2))  3.5 us
    transpose x1, local copies, waits for them, and re-layouts, local(): return jnp.transpose(result, (1, 0, 2))  2.87 us

profile of v2, /device:TPU:1, one launch (start us, length us, event | category | flops | bytes accessed | tf_op | source)
XLA Modules:
  0.0 78.5 jit_solution(8285444963352162850)
XLA Ops:
  0.7 3.5 %copy_bitcast_fusion = (f32[4,128,512]{2,1,0:T(8,128)}, f32[4,128,512]{2,1,0:T(8,128)}) fusion(f32[128,4,512]{2,1,0:T(4,128)} %param.6, f32[128,4,512]{2,1,0:T(4,128)} %param.5), kind=kLoop, calls=%fused_computation | loop fusion | bytes 4194304 | tf_op jit(solution)/shard_map/transpose | solution.py:273
  4.1 71.4 %shard_map.55 = f32[4,128,512]{2,1,0:T(8,128)} custom-call(f32[4,128,512]{2,1,0:T(8,128)} %get-tuple-element.6.temp, f32[4,128,512]{2,1,0:T(8,128)} %get-tuple-element.5.source, f32[1,128]{1,0:T(1,128)} %bitcast.7, f32[1]{0:T(128)S(6)} %copy.11.face, f32[128,128]{1,0:T(8,128)} %inverse.1), custom_call_target="tpu_custom_call" | custom-call | tf_op jit(solution)/shard_map/pallas_call | solution.py:249
  75.6 2.9 %copy.8 = f32[128,4,512]{2,1,0:T(4,128)} copy(f32[128,4,512]{2,0,1:T(8,128)} %bitcast.6) | data formatting | bytes 2097152 | tf_op jit(solution)/shard_map/transpose | solution.py:276
